TPU v7x, 32 devices: a whole 2x2x4 slice. The times are simulated.
32 devices in a mesh: node: 32 (over z, y, x, core).
Axes of the slice: x: 2, y: 2, z: 4, core: 2. Of those that a mesh axis runs over, the one named last changes fastest.
Arguments:
- round_index: int32 [1], replicated, may hold values from 0 to 63
- sample_ids: int32 [32, 8], P('node'), may hold values from 0 to 3
- token_pool: bfloat16 [32, 4, 64, 512], P('node'), may hold values from -20 to 20
- cotangent_pool: bfloat16 [32, 4, 64, 512], P('node'), may hold values from -6 to 6
- weights: bfloat16 [32, 4, 512, 512], P('node'), may hold values from -12 to 12
- residue: bfloat16 [32, 4, 512, 512], P('node'), may hold values from -6 to 6
Outputs:
- new_weights: bfloat16 [32, 4, 512, 512], P('node')
- new_residue: bfloat16 [32, 4, 512, 512], P('node')
- grad_rms: float32 [], replicated
All inputs are finite; a program needn't handle non-finite values.
Results may differ from a plain program's by a relative error of at most 0.0065.
Values may be sent and summed in bfloat16 or wider, within the bound.
A program may use at most 128 MiB of HBM per device.

v0:
```python
from functools import partial

import jax
import jax.numpy as jnp
from jax import lax
from jax.experimental import pallas as pl
from jax.experimental.pallas import tpu as pltpu
from jax.sharding import PartitionSpec as P

HEAD_DIM = 64
LANES = 128
CHUNK_ROWS = 128

epsilon = 1e-06
step_rate = 0.1

f32, bf16 = jnp.float32, jnp.bfloat16
MESH = pl.DeviceIdType.MESH
VMEM = pl.BlockSpec(memory_space=pltpu.VMEM)
SMEM = pl.BlockSpec(memory_space=pltpu.SMEM)
HBM = pl.BlockSpec(memory_space=pl.ANY)


def dot(left, right, left_dim=1, right_dim=0):
    return lax.dot_general(
        left, right, (((left_dim,), (right_dim,)), ((), ())), preferred_element_type=f32
    )


def round_kernel(
    nodes,
    offset,
    ids_ref,
    tokens_hbm,
    cot_hbm,
    weights_hbm,
    residue_hbm,
    new_weights_ref,
    new_residue_ref,
    rms_ref,
    tokens_ref,
    cot_ref,
    weights_ref,
    residue_ref,
    left_ref,
    right_ref,
    context_ref,
    gradient,
    tracked,
    tracked_in,
    sent,
    sent_in,
    squares,
    totals,
    totals_in,
    load_sems,
    track_send,
    track_recv,
    sent_send,
    sent_recv,
    sum_send,
    sum_recv,
):
    me = lax.axis_index("node")
    target = lax.rem(me + offset, nodes)
    source = lax.rem(me + nodes - offset, nodes)
    steps = nodes.bit_length() - 1
    mutual = 2 * offset == nodes
    strides = [2**k for k in range(steps)]
    if not mutual:
        strides = [offset] + [stride for stride in strides if stride != offset]
    partners = [me + stride * (1 - 2 * ((me // stride) % 2)) for stride in strides]

    barrier = pltpu.get_barrier_semaphore()
    for other in [target, source] + partners:
        pl.semaphore_signal(barrier, inc=1, device_id=(other,), device_id_type=MESH)

    pool, seq, width = tokens_ref.shape
    matrices = weights_ref.shape[0]
    batch = ids_ref.shape[1]
    rows = pool * seq
    pairs = width // LANES
    per_matrix = width // CHUNK_ROWS
    proj_scale = width**-0.5
    head_scale = HEAD_DIM**-0.5
    order = [3, 2, 0, 1]

    moves = {"tokens": (tokens_hbm.at[0], tokens_ref), "cot": (cot_hbm.at[0], cot_ref)}
    for m in range(matrices):
        moves["w", m] = (weights_hbm.at[0, m], weights_ref.at[m])
        moves["r", m] = (residue_hbm.at[0, m], residue_ref.at[m])
    when = ["tokens", ("w", 0), ("w", 1), ("w", 2), "cot", ("r", 3), ("w", 3), ("r", 2), ("r", 0), ("r", 1)]
    loads = {name: pltpu.make_async_copy(*moves[name], load_sems.at[n]) for n, name in enumerate(when)}
    for name in when:
        loads[name].start()

    def track_copy(c):
        return pltpu.make_async_remote_copy(
            tracked.at[c], tracked_in.at[c], track_send.at[c], track_recv.at[c], (target,), MESH
        )

    def sent_copy(c):
        return pltpu.make_async_remote_copy(
            sent.at[c], sent_in.at[c], sent_send.at[c], sent_recv.at[c], (target,), MESH
        )

    def weights_copy(m, part, c):
        return pltpu.make_async_remote_copy(
            weights_hbm.at[0, m, part],
            sent_in.at[c],
            sent_send.at[c],
            sent_recv.at[c],
            (target,),
            MESH,
        )

    def each_block(which, body):
        for m in which:

            @pl.loop(0, per_matrix)
            def _(r):
                body(m, pl.ds(r * CHUNK_ROWS, CHUNK_ROWS), order.index(m) * per_matrix + r)

    def send_weights(m, part, c):
        weights_copy(m, part, c).start()

    if mutual:
        pl.semaphore_wait(barrier, 2 + steps)
        each_block(order[:2], send_weights)

    counts = []
    for image in range(pool):
        count = jnp.int32(0)
        for draw in range(batch):
            count = count + (ids_ref[0, draw] == image).astype(jnp.int32)
        counts.append(count.astype(f32))

    loads["tokens"].wait()
    values = tokens_ref[...].reshape(rows, width).astype(f32)
    centered = values - jnp.mean(values, -1, keepdims=True)
    variance = jnp.mean(centered * centered, -1, keepdims=True)
    unit_rows = centered * lax.rsqrt(variance + epsilon)
    normed = unit_rows.astype(bf16)
    first = lax.broadcasted_iota(jnp.int32, (seq, LANES), 1) < HEAD_DIM
    units = [(i, j) for i in range(pool) for j in range(pairs)]
    spots = [
        (slice(i * seq, (i + 1) * seq), slice(j * LANES, (j + 1) * LANES)) for i, j in units
    ]

    def spread(block):
        zero = jnp.zeros_like(block)
        return jnp.concatenate([jnp.where(first, block, zero), jnp.where(first, zero, block)], 0)

    def gather(block):
        return jnp.where(first, block[:seq], block[seq:])

    def track(m, part, c):
        right = right_ref[m] if m < 3 else cot_ref[...].reshape(rows, width)
        grad = dot(left_ref[m // 3, part], right) * proj_scale
        gradient[c] = grad
        tracked[c] = (residue_ref[m, part].astype(f32) + grad).astype(bf16)
        track_copy(c).start()
        squares[...] += jnp.sum((grad * grad).reshape(-1, 8, width), 0)

    squares[...] = jnp.zeros_like(squares)
    for m in range(3):
        loads["w", m].wait()
    loads["cot"].wait()
    loads["r", 3].wait()
    queries2, keys1, vals1, probs, half = {}, {}, {}, {}, {}
    for j in range(pairs):
        cols = slice(j * LANES, (j + 1) * LANES)
        queries, keys, vals = [
            (dot(normed, weights_ref[m, :, cols]) * proj_scale).astype(bf16) for m in range(3)
        ]
        here = [(i, j) for i in range(pool)]
        for i, u in enumerate(here):
            part = slice(i * seq, (i + 1) * seq)
            queries2[u], keys1[u], vals1[u] = spread(queries[part]), keys[part], vals[part]
        scores = [dot(queries2[u], keys1[u], 1, 1) * head_scale for u in here]
        for u, score in zip(here, scores):
            e = jnp.exp(score - jnp.max(score, -1, keepdims=True))
            probs[u] = e / jnp.sum(e, -1, keepdims=True)
            half[u] = probs[u].astype(bf16)
        context = [gather(dot(half[u], vals1[u])) * counts[u[0]] for u in here]
        left_ref[1, cols] = jnp.concatenate(context, 0).T.astype(bf16)
        if j == 0 and not mutual:
            pl.semaphore_wait(barrier, 2 + steps)
        track(3, pl.ds(j * LANES, LANES), order.index(3) * per_matrix + j)

    loads["w", 3].wait()
    cot = cot_ref[...].reshape(rows, width)
    context_grad = (dot(cot, weights_ref[3], 1, 1) * proj_scale).astype(bf16)
    weighted = [unit_rows[i * seq : (i + 1) * seq] * counts[i] for i in range(pool)]
    left_ref[0] = jnp.concatenate(weighted, 0).T.astype(bf16)
    queries2, keys1, vals1, probs, half = [
        [found[u] for u in units] for found in (queries2, keys1, vals1, probs, half)
    ]
    grads2 = [spread(context_grad[at]) for at in spots]
    for n, at in enumerate(spots):
        right_ref[2, at[0], at[1]] = dot(half[n], grads2[n], 0, 0).astype(bf16)
    probs_grad = [dot(g, v, 1, 1) for g, v in zip(grads2, vals1)]
    score_grad = []
    for p, g in zip(probs, probs_grad):
        inner = jnp.sum(g * p, -1, keepdims=True)
        score_grad.append((p * (g - inner) * head_scale).astype(bf16))
    for n, at in enumerate(spots):
        right_ref[0, at[0], at[1]] = gather(dot(score_grad[n], keys1[n])).astype(bf16)
        right_ref[1, at[0], at[1]] = dot(score_grad[n], queries2[n], 0, 0).astype(bf16)
    for m in order[1:]:
        loads["r", m].wait()
    each_block(order[1:], track)

    def sum_copy(k):
        return pltpu.make_async_remote_copy(
            totals.at[k], totals_in.at[k], sum_send.at[k], sum_recv.at[k], (partners[k],), MESH
        )

    def sum_finish(k):
        sum_copy(k).wait()
        totals[k + 1] = totals[k] + totals_in[k]

    own_total = jnp.sum(jnp.sum(squares[...], 0, keepdims=True), 1, keepdims=True)
    totals[0] = jnp.broadcast_to(own_total, totals.shape[1:])
    entries = nodes * matrices * width * width

    def set_rms():
        rms_ref[0] = jnp.max(jnp.sqrt(totals[steps] / entries))

    def mix(m, part, c):
        track_copy(c).wait_recv()
        tracker = 0.5 * (tracked[c].astype(f32) + tracked_in[c].astype(f32))
        own = weights_ref[m, part].astype(f32)
        new_residue_ref[0, m, part] = (tracker - gradient[c]).astype(bf16)
        base = 0.5 * own - 0.5 * step_rate * tracker
        if mutual:
            weights_copy(m, part, c).wait_recv()
            peer_sent = (sent_in[c].astype(f32) - step_rate * tracker).astype(bf16)
            new_weights_ref[0, m, part] = (base + 0.5 * peer_sent.astype(f32)).astype(bf16)
        else:
            sent[c] = (own - step_rate * tracker).astype(bf16)
            sent_copy(c).start()
            gradient[c] = base

    def finish(m, part, c):
        sent_copy(c).wait_recv()
        new_weights_ref[0, m, part] = (gradient[c] + 0.5 * sent_in[c].astype(f32)).astype(bf16)

    def drain(m, part, c):
        track_copy(c).wait_send()
        (weights_copy(m, part, c) if mutual else sent_copy(c)).wait_send()

    if mutual:
        for k in range(steps - 2):
            sum_copy(k).start()
            sum_finish(k)
        for n, k in enumerate([steps - 2, steps - 1]):
            sum_copy(k).start()
            each_block([order[2 + n]], send_weights)
            each_block([order[n]], mix)
            sum_finish(k)
        set_rms()
        each_block(order[2:], mix)
    else:
        sum_copy(0).start()
        each_block(order, mix)
        sum_finish(0)
        spans = len(order) - 1
        for at, m in enumerate(order[:-1]):
            here = range(1 + (steps - 1) * at // spans, 1 + (steps - 1) * (at + 1) // spans)
            for k in here:
                sum_copy(k).start()
                if k != here[-1]:
                    sum_finish(k)
            each_block([m], finish)
            if here:
                sum_finish(here[-1])
        set_rms()
        each_block(order[-1:], finish)
    each_block(order, drain)


def one_round(nodes, level, sample_ids, token_pool, cotangent_pool, weights, residue):
    pool, seq, width = token_pool.shape[1:]
    matrices = weights.shape[1]
    rows = pool * seq
    chunks = matrices * (width // CHUNK_ROWS)
    steps = nodes.bit_length() - 1
    chunked = (chunks, CHUNK_ROWS, width)
    dma = pltpu.SemaphoreType.DMA
    return pl.pallas_call(
        partial(round_kernel, nodes, 2**level),
        out_shape=(
            jax.ShapeDtypeStruct(weights.shape, bf16),
            jax.ShapeDtypeStruct(weights.shape, bf16),
            jax.ShapeDtypeStruct((1,), f32),
        ),
        in_specs=[SMEM] + [HBM] * 4,
        out_specs=(VMEM, VMEM, SMEM),
        scratch_shapes=[
            pltpu.VMEM((pool, seq, width), bf16),
            pltpu.VMEM((pool, seq, width), bf16),
            pltpu.VMEM(weights.shape[1:], bf16),
            pltpu.VMEM(weights.shape[1:], bf16),
            pltpu.VMEM((2, width, rows), bf16),
            pltpu.VMEM((3, rows, width), bf16),
            pltpu.VMEM((rows, width), f32),
            pltpu.VMEM(chunked, f32),
            pltpu.VMEM(chunked, bf16),
            pltpu.VMEM(chunked, bf16),
            pltpu.VMEM(chunked, bf16),
            pltpu.VMEM(chunked, bf16),
            pltpu.VMEM((8, width), f32),
            pltpu.VMEM((steps + 1, 8, LANES), f32),
            pltpu.VMEM((steps, 8, LANES), f32),
            dma((2 + 2 * matrices,)),
            dma((chunks,)),
            dma((chunks,)),
            dma((chunks,)),
            dma((chunks,)),
            dma((steps,)),
            dma((steps,)),
        ],
        compiler_params=pltpu.CompilerParams(
            collective_id=level, has_side_effects=True, vmem_limit_bytes=40 * 2**20
        ),
    )(sample_ids, token_pool, cotangent_pool, weights, residue)


def write_kernel(weights_ref, residue_ref, weights_out, residue_out, sems):
    copies = []
    for n, (src, dst) in enumerate([(weights_ref, weights_out), (residue_ref, residue_out)]):
        for m in range(src.shape[1]):
            copies.append(pltpu.make_async_copy(src.at[0, m], dst.at[0, m], sems.at[n, m]))
    for copy in copies:
        copy.start()
    for copy in copies:
        copy.wait()


def write_out(new_weights, new_residue):
    shape = jax.ShapeDtypeStruct(new_weights.shape, bf16)
    return pl.pallas_call(
        write_kernel,
        out_shape=(shape, shape),
        in_specs=[VMEM, VMEM],
        out_specs=(HBM, HBM),
        scratch_shapes=[pltpu.SemaphoreType.DMA((2, new_weights.shape[1]))],
        compiler_params=pltpu.CompilerParams(vmem_limit_bytes=8 * 2**20),
    )(new_weights, new_residue)


def per_device(round_index, sample_ids, token_pool, cotangent_pool, weights, residue):
    nodes = lax.axis_size("node")
    levels = nodes.bit_length() - 1
    new_weights, new_residue, grad_rms = lax.switch(
        round_index[0] % levels,
        [partial(one_round, nodes, level) for level in range(levels)],
        sample_ids,
        token_pool,
        cotangent_pool,
        weights,
        residue,
    )
    new_weights, new_residue = write_out(new_weights, new_residue)
    return (new_weights, new_residue, grad_rms[0])


def solution(mesh):
    placed = (
        P(),
        P("node", None),
        P("node", None, None, None),
        P("node", None, None, None),
        P("node", None, None, None),
        P("node", None, None, None),
    )
    return jax.shard_map(
        per_device,
        mesh=mesh,
        in_specs=placed,
        out_specs=(P("node", None, None, None), P("node", None, None, None), P()),
        check_vma=False,
    )
```

profile of v0, /device:TPU:0, one launch (start us, length us, event | category | flops | bytes accessed | tf_op | source)
XLA Modules:
  0.0 107.0 jit_solution(4777488110313916023)
XLA Ops:
  1.3 102.0 %conditional.1 = (bf16[1,4,512,512]{3,2,1,0:T(8,128)(2,1)S(1)}, bf16[1,4,512,512]{3,2,1,0:T(8,128)(2,1)S(1)}, f32[]{:T(128)}) conditional(s32[]{:T(128)} %clamp.3, (s32[1,8]{1,0:T(1,128)}, bf16[1,4,64,512]{3,2,1,0:T(8,128)(2,1)}, bf16[1,4,64,512]{3,2,1,0:T(8,128)(2,1)}, bf16[1,4,512,512]{3,2,1,0:T(8,128)(2,1)}, ...), branch_computations={%region_0.1_spmd, %region_1.2_spmd, %region_2.3_spmd, %region_3.4_... | conditional | bytes 24 | solution.py:356
  1.5 101.6 %branch_2_fun.1 = (bf16[1,4,512,512]{3,2,1,0:T(8,128)(2,1)S(1)}, bf16[1,4,512,512]{3,2,1,0:T(8,128)(2,1)S(1)}, f32[1]{0:T(128)}) custom-call(s32[1,8]{1,0:T(1,128)} %get-tuple-element.82.ids_ref, bf16[1,4,64,512]{3,2,1,0:T(8,128)(2,1)} %get-tuple-element.83.tokens_hbm, bf16[1,4,64,512]{3,2,1,0:T(8,128)(2,1)} %get-tuple-element.84.cot_hbm, ...), custom_call_target="tpu_custom_call" | custom-call | tf_op jit(solution)/shard_map/cond/branch_2_fun/pallas_call | solution.py:291
  103.3 2.1 %shard_map.85 = (bf16[1,4,512,512]{3,2,1,0:T(8,128)(2,1)}, bf16[1,4,512,512]{3,2,1,0:T(8,128)(2,1)}) custom-call(bf16[1,4,512,512]{3,2,1,0:T(8,128)(2,1)S(1)} %get-tuple-element.114.weights_ref, bf16[1,4,512,512]{3,2,1,0:T(8,128)(2,1)S(1)} %get-tuple-element.115.residue_ref), custom_call_target="tpu_custom_call" | custom-call | tf_op jit(solution)/shard_map/pallas_call | solution.py:343
where the time goes:
time: 107 us
  Pallas kernels  104 us (97%)
  between operations  2.99 us (3%)
    pallas_call x1, Pallas kernels, one_round(): pl.pallas_call(partial(round_kernel, nodes, 2 ** level), out_shape=(jax.S...  102 us

commit v1 on v0

--- a/solution.py
+++ b/solution.py
@@ -17,8 +17,7 @@
 f32, bf16 = jnp.float32, jnp.bfloat16
 MESH = pl.DeviceIdType.MESH
 VMEM = pl.BlockSpec(memory_space=pltpu.VMEM)
-SMEM = pl.BlockSpec(memory_space=pltpu.SMEM)
-HBM = pl.BlockSpec(memory_space=pl.ANY)
+HBM = pl.BlockSpec(memory_space=pltpu.HBM)
 
 
 def dot(left, right, left_dim=1, right_dim=0):
@@ -30,7 +29,7 @@
 def round_kernel(
     nodes,
     offset,
-    ids_ref,
+    ids_hbm,
     tokens_hbm,
     cot_hbm,
     weights_hbm,
@@ -38,6 +37,7 @@
     new_weights_ref,
     new_residue_ref,
     rms_ref,
+    ids_ref,
     tokens_ref,
     cot_ref,
     weights_ref,
@@ -77,7 +77,6 @@
 
     pool, seq, width = tokens_ref.shape
     matrices = weights_ref.shape[0]
-    batch = ids_ref.shape[1]
     rows = pool * seq
     pairs = width // LANES
     per_matrix = width // CHUNK_ROWS
@@ -86,10 +85,18 @@
     order = [3, 2, 0, 1]
 
     moves = {"tokens": (tokens_hbm.at[0], tokens_ref), "cot": (cot_hbm.at[0], cot_ref)}
-    for m in range(matrices):
-        moves["w", m] = (weights_hbm.at[0, m], weights_ref.at[m])
+    moves["ids"] = (ids_hbm, ids_ref)
+    head_cols, rest_cols = pl.ds(0, LANES), pl.ds(LANES, width - LANES)
+    head_rows, rest_rows = pl.ds(0, CHUNK_ROWS), pl.ds(CHUNK_ROWS, width - CHUNK_ROWS)
+    for m in range(3):
+        moves["w", m] = (weights_hbm.at[0, m, :, head_cols], weights_ref.at[m, :, head_cols])
+        moves["w+", m] = (weights_hbm.at[0, m, :, rest_cols], weights_ref.at[m, :, rest_cols])
         moves["r", m] = (residue_hbm.at[0, m], residue_ref.at[m])
-    when = ["tokens", ("w", 0), ("w", 1), ("w", 2), "cot", ("r", 3), ("w", 3), ("r", 2), ("r", 0), ("r", 1)]
+    moves["w", 3] = (weights_hbm.at[0, 3], weights_ref.at[3])
+    moves["r", 3] = (residue_hbm.at[0, 3, head_rows], residue_ref.at[3, head_rows])
+    moves["r+", 3] = (residue_hbm.at[0, 3, rest_rows], residue_ref.at[3, rest_rows])
+    when = ["tokens", ("w", 0), ("w", 1), ("w", 2), "ids", "cot", ("r", 3), ("w+", 0), ("w+", 1), ("w+", 2), ("r+", 3)]
+    when += [("w", 3), ("r", 2), ("r", 0), ("r", 1)]
     loads = {name: pltpu.make_async_copy(*moves[name], load_sems.at[n]) for n, name in enumerate(when)}
     for name in when:
         loads[name].start()
@@ -127,13 +134,6 @@
     if mutual:
         pl.semaphore_wait(barrier, 2 + steps)
         each_block(order[:2], send_weights)
-
-    counts = []
-    for image in range(pool):
-        count = jnp.int32(0)
-        for draw in range(batch):
-            count = count + (ids_ref[0, draw] == image).astype(jnp.int32)
-        counts.append(count.astype(f32))
 
     loads["tokens"].wait()
     values = tokens_ref[...].reshape(rows, width).astype(f32)
@@ -155,21 +155,26 @@
         return jnp.where(first, block[:seq], block[seq:])
 
     def track(m, part, c):
-        right = right_ref[m] if m < 3 else cot_ref[...].reshape(rows, width)
+        right = right_ref[m] if m < 3 else cot
         grad = dot(left_ref[m // 3, part], right) * proj_scale
         gradient[c] = grad
         tracked[c] = (residue_ref[m, part].astype(f32) + grad).astype(bf16)
-        track_copy(c).start()
+        if mutual or m in order[:2]:
+            track_copy(c).start()
         squares[...] += jnp.sum((grad * grad).reshape(-1, 8, width), 0)
 
+    loads["ids"].wait()
+    ids = ids_ref[...]
+    counts = [jnp.sum((ids == image).astype(f32), 1, keepdims=True) for image in range(pool)]
+    loads["cot"].wait()
+    cot = cot_ref[...].reshape(rows, width)
     squares[...] = jnp.zeros_like(squares)
-    for m in range(3):
-        loads["w", m].wait()
-    loads["cot"].wait()
-    loads["r", 3].wait()
     queries2, keys1, vals1, probs, half = {}, {}, {}, {}, {}
     for j in range(pairs):
         cols = slice(j * LANES, (j + 1) * LANES)
+        if j < 2:
+            for m in range(3):
+                loads["w+" if j else "w", m].wait()
         queries, keys, vals = [
             (dot(normed, weights_ref[m, :, cols]) * proj_scale).astype(bf16) for m in range(3)
         ]
@@ -186,10 +191,11 @@
         left_ref[1, cols] = jnp.concatenate(context, 0).T.astype(bf16)
         if j == 0 and not mutual:
             pl.semaphore_wait(barrier, 2 + steps)
+        if j < 2:
+            loads["r+" if j else "r", 3].wait()
         track(3, pl.ds(j * LANES, LANES), order.index(3) * per_matrix + j)
 
     loads["w", 3].wait()
-    cot = cot_ref[...].reshape(rows, width)
     context_grad = (dot(cot, weights_ref[3], 1, 1) * proj_scale).astype(bf16)
     weighted = [unit_rows[i * seq : (i + 1) * seq] * counts[i] for i in range(pool)]
     left_ref[0] = jnp.concatenate(weighted, 0).T.astype(bf16)
@@ -199,6 +205,8 @@
     grads2 = [spread(context_grad[at]) for at in spots]
     for n, at in enumerate(spots):
         right_ref[2, at[0], at[1]] = dot(half[n], grads2[n], 0, 0).astype(bf16)
+    loads["r", 2].wait()
+    each_block([2], track)
     probs_grad = [dot(g, v, 1, 1) for g, v in zip(grads2, vals1)]
     score_grad = []
     for p, g in zip(probs, probs_grad):
@@ -207,9 +215,9 @@
     for n, at in enumerate(spots):
         right_ref[0, at[0], at[1]] = gather(dot(score_grad[n], keys1[n])).astype(bf16)
         right_ref[1, at[0], at[1]] = dot(score_grad[n], queries2[n], 0, 0).astype(bf16)
-    for m in order[1:]:
+    for m in order[2:]:
         loads["r", m].wait()
-    each_block(order[1:], track)
+    each_block(order[2:], track)
 
     def sum_copy(k):
         return pltpu.make_async_remote_copy(
@@ -225,7 +233,7 @@
     entries = nodes * matrices * width * width
 
     def set_rms():
-        rms_ref[0] = jnp.max(jnp.sqrt(totals[steps] / entries))
+        rms_ref[0] = jnp.sqrt(totals[steps] / entries)
 
     def mix(m, part, c):
         track_copy(c).wait_recv()
@@ -248,7 +256,10 @@
 
     def drain(m, part, c):
         track_copy(c).wait_send()
-        (weights_copy(m, part, c) if mutual else sent_copy(c)).wait_send()
+        weights_copy(m, part, c).wait_send()
+
+    def drain_sent(m, part, c):
+        sent_copy(c).wait_send()
 
     if mutual:
         for k in range(steps - 2):
@@ -261,23 +272,28 @@
             sum_finish(k)
         set_rms()
         each_block(order[2:], mix)
+        each_block(order, drain)
     else:
-        sum_copy(0).start()
+        chunks = matrices * per_matrix
+        held = 2 * per_matrix
+        lag = min(3, held)
+        starts = [held + k * (chunks - held) // steps for k in range(steps)]
+        for c in range(held, chunks):
+            track_copy(c - lag).wait_send()
+            for k in range(steps):
+                if starts[k] == c:
+                    if k:
+                        sum_finish(k - 1)
+                    sum_copy(k).start()
+            track_copy(c).start()
+        sum_finish(steps - 1)
+        set_rms()
         each_block(order, mix)
-        sum_finish(0)
-        spans = len(order) - 1
-        for at, m in enumerate(order[:-1]):
-            here = range(1 + (steps - 1) * at // spans, 1 + (steps - 1) * (at + 1) // spans)
-            for k in here:
-                sum_copy(k).start()
-                if k != here[-1]:
-                    sum_finish(k)
-            each_block([m], finish)
-            if here:
-                sum_finish(here[-1])
-        set_rms()
-        each_block(order[-1:], finish)
-    each_block(order, drain)
+        each_block(order, finish)
+        for c in range(chunks):
+            if c < held - lag or c >= chunks - lag:
+                track_copy(c).wait_send()
+        each_block(order, drain_sent)
 
 
 def one_round(nodes, level, sample_ids, token_pool, cotangent_pool, weights, residue):
@@ -288,16 +304,17 @@
     steps = nodes.bit_length() - 1
     chunked = (chunks, CHUNK_ROWS, width)
     dma = pltpu.SemaphoreType.DMA
-    return pl.pallas_call(
+    new_weights, new_residue, grad_rms = pl.pallas_call(
         partial(round_kernel, nodes, 2**level),
         out_shape=(
             jax.ShapeDtypeStruct(weights.shape, bf16),
             jax.ShapeDtypeStruct(weights.shape, bf16),
-            jax.ShapeDtypeStruct((1,), f32),
+            jax.ShapeDtypeStruct((1, 8, LANES), f32),
         ),
-        in_specs=[SMEM] + [HBM] * 4,
-        out_specs=(VMEM, VMEM, SMEM),
+        in_specs=[HBM] * 5,
+        out_specs=(VMEM, VMEM, VMEM),
         scratch_shapes=[
+            pltpu.VMEM(sample_ids.shape, jnp.int32),
             pltpu.VMEM((pool, seq, width), bf16),
             pltpu.VMEM((pool, seq, width), bf16),
             pltpu.VMEM(weights.shape[1:], bf16),
@@ -313,7 +330,7 @@
             pltpu.VMEM((8, width), f32),
             pltpu.VMEM((steps + 1, 8, LANES), f32),
             pltpu.VMEM((steps, 8, LANES), f32),
-            dma((2 + 2 * matrices,)),
+            dma((7 + 2 * matrices,)),
             dma((chunks,)),
             dma((chunks,)),
             dma((chunks,)),
@@ -322,32 +339,37 @@
             dma((steps,)),
         ],
         compiler_params=pltpu.CompilerParams(
-            collective_id=level, has_side_effects=True, vmem_limit_bytes=40 * 2**20
+            collective_id=level, has_side_effects=True, vmem_limit_bytes=30 * 2**20
         ),
     )(sample_ids, token_pool, cotangent_pool, weights, residue)
-
-
-def write_kernel(weights_ref, residue_ref, weights_out, residue_out, sems):
+    return new_weights, new_residue, grad_rms[0]
+
+
+def write_kernel(weights_ref, residue_ref, rms_ref, weights_out, residue_out, rms_out, rms, rms_sem, sems):
     copies = []
     for n, (src, dst) in enumerate([(weights_ref, weights_out), (residue_ref, residue_out)]):
         for m in range(src.shape[1]):
             copies.append(pltpu.make_async_copy(src.at[0, m], dst.at[0, m], sems.at[n, m]))
     for copy in copies:
         copy.start()
+    rms[0] = rms_ref[0, 0]
+    copies.append(pltpu.make_async_copy(rms, rms_out, rms_sem))
+    copies[-1].start()
     for copy in copies:
         copy.wait()
 
 
-def write_out(new_weights, new_residue):
+def write_out(new_weights, new_residue, grad_rms):
     shape = jax.ShapeDtypeStruct(new_weights.shape, bf16)
+    dma = pltpu.SemaphoreType.DMA
     return pl.pallas_call(
         write_kernel,
-        out_shape=(shape, shape),
-        in_specs=[VMEM, VMEM],
-        out_specs=(HBM, HBM),
-        scratch_shapes=[pltpu.SemaphoreType.DMA((2, new_weights.shape[1]))],
+        out_shape=(shape, shape, jax.ShapeDtypeStruct((1,), f32)),
+        in_specs=[VMEM, VMEM, VMEM],
+        out_specs=(HBM, HBM, HBM),
+        scratch_shapes=[pltpu.SMEM((1,), f32), dma, dma((2, new_weights.shape[1]))],
         compiler_params=pltpu.CompilerParams(vmem_limit_bytes=8 * 2**20),
-    )(new_weights, new_residue)
+    )(new_weights, new_residue, grad_rms)
 
 
 def per_device(round_index, sample_ids, token_pool, cotangent_pool, weights, residue):
@@ -362,7 +384,7 @@
         weights,
         residue,
     )
-    new_weights, new_residue = write_out(new_weights, new_residue)
+    new_weights, new_residue, grad_rms = write_out(new_weights, new_residue, grad_rms)
     return (new_weights, new_residue, grad_rms[0])
 
 

time: 107 us -> 104 us (0.972)
  Pallas kernels: 104 us -> 102 us
  between operations: 2.99 us -> 1.48 us
    pallas_call x1, Pallas kernels: 102 us -> 100 us  [one_round(): pl.pallas_call(partial(round_kernel, nodes, 2 ** level), out_shape=(jax.S...]
where the time goes in v1:
time: 104 us
  Pallas kernels  102 us (98%)
  between operations  1.48 us (1%)
    pallas_call x1, Pallas kernels, one_round(): pl.pallas_call(partial(round_kernel, nodes, 2 ** level), out_shape=(jax.S...  100 us
    pallas_call x1, Pallas kernels, write_out(): pl.pallas_call(write_kernel, out_shape=(shape, shape, jax.ShapeDtypeStruc...  2.09 us

profile of v1, /device:TPU:0, one launch (start us, length us, event | category | flops | bytes accessed | tf_op | source)
XLA Modules:
  0.0 104.1 jit_solution(6591074480878790713)
XLA Ops:
  1.3 100.5 %conditional.1 = (bf16[1,4,512,512]{3,2,1,0:T(8,128)(2,1)S(1)}, bf16[1,4,512,512]{3,2,1,0:T(8,128)(2,1)S(1)}, f32[8,128]{1,0:T(8,128)S(1)}) conditional(s32[]{:T(128)} %clamp.3, (s32[1,8]{1,0:T(1,128)}, bf16[1,4,64,512]{3,2,1,0:T(8,128)(2,1)}, bf16[1,4,64,512]{3,2,1,0:T(8,128)(2,1)}, ...), branch_computations={%region_0.1_spmd, %region_1.2_spmd, %region_2.3_spmd, %region_3.4_... | conditional | bytes 24 | solution.py:378
  1.5 100.1 %branch_2_fun.1 = (bf16[1,4,512,512]{3,2,1,0:T(8,128)(2,1)S(1)}, bf16[1,4,512,512]{3,2,1,0:T(8,128)(2,1)S(1)}, f32[1,8,128]{2,1,0:T(8,128)S(1)}) custom-call(s32[1,8]{1,0:T(1,128)} %get-tuple-element.66.ids_hbm, bf16[1,4,64,512]{3,2,1,0:T(8,128)(2,1)} %get-tuple-element.67.tokens_hbm, bf16[1,4,64,512]{3,2,1,0:T(8,128)(2,1)} %get-tuple-element.68.cot_hbm, ...), custom_call_target="tpu_custom_call" | custom-call | tf_op jit(solution)/shard_map/cond/branch_2_fun/pallas_call | solution.py:307
  101.8 2.1 %shard_map.85 = (bf16[1,4,512,512]{3,2,1,0:T(8,128)(2,1)}, bf16[1,4,512,512]{3,2,1,0:T(8,128)(2,1)}, f32[1]{0:T(128)}) custom-call(bf16[1,4,512,512]{3,2,1,0:T(8,128)(2,1)S(1)} %get-tuple-element.99.weights_ref, bf16[1,4,512,512]{3,2,1,0:T(8,128)(2,1)S(1)} %get-tuple-element.100.residue_ref, f32[8,128]{1,0:T(8,128)S(1)} %get-tuple-element.101.rms_ref), custom_call_target="tpu_custom_call" | custom-call | tf_op jit(solution)/shard_map/pallas_call | solution.py:365

commit v2 on v1

--- a/solution.py
+++ b/solution.py
@@ -10,6 +10,7 @@
 HEAD_DIM = 64
 LANES = 128
 CHUNK_ROWS = 128
+LAG = 3
 
 epsilon = 1e-06
 step_rate = 0.1
@@ -71,55 +72,90 @@
         strides = [offset] + [stride for stride in strides if stride != offset]
     partners = [me + stride * (1 - 2 * ((me // stride) % 2)) for stride in strides]
 
-    barrier = pltpu.get_barrier_semaphore()
-    for other in [target, source] + partners:
-        pl.semaphore_signal(barrier, inc=1, device_id=(other,), device_id_type=MESH)
-
     pool, seq, width = tokens_ref.shape
     matrices = weights_ref.shape[0]
     rows = pool * seq
     pairs = width // LANES
     per_matrix = width // CHUNK_ROWS
+    chunks = matrices * per_matrix
     proj_scale = width**-0.5
     head_scale = HEAD_DIM**-0.5
     order = [3, 2, 0, 1]
 
-    moves = {"tokens": (tokens_hbm.at[0], tokens_ref), "cot": (cot_hbm.at[0], cot_ref)}
-    moves["ids"] = (ids_hbm, ids_ref)
+    head, rest = pl.ds(0, CHUNK_ROWS), pl.ds(CHUNK_ROWS, width - CHUNK_ROWS)
     head_cols, rest_cols = pl.ds(0, LANES), pl.ds(LANES, width - LANES)
-    head_rows, rest_rows = pl.ds(0, CHUNK_ROWS), pl.ds(CHUNK_ROWS, width - CHUNK_ROWS)
-    for m in range(3):
-        moves["w", m] = (weights_hbm.at[0, m, :, head_cols], weights_ref.at[m, :, head_cols])
-        moves["w+", m] = (weights_hbm.at[0, m, :, rest_cols], weights_ref.at[m, :, rest_cols])
-        moves["r", m] = (residue_hbm.at[0, m], residue_ref.at[m])
-    moves["w", 3] = (weights_hbm.at[0, 3], weights_ref.at[3])
-    moves["r", 3] = (residue_hbm.at[0, 3, head_rows], residue_ref.at[3, head_rows])
-    moves["r+", 3] = (residue_hbm.at[0, 3, rest_rows], residue_ref.at[3, rest_rows])
-    when = ["tokens", ("w", 0), ("w", 1), ("w", 2), "ids", "cot", ("r", 3), ("w+", 0), ("w+", 1), ("w+", 2), ("r+", 3)]
-    when += [("w", 3), ("r", 2), ("r", 0), ("r", 1)]
-    loads = {name: pltpu.make_async_copy(*moves[name], load_sems.at[n]) for n, name in enumerate(when)}
-    for name in when:
+    qkv, pair = pl.ds(0, 3), pl.ds(0, 2)
+    moves = {
+        "tokens": (tokens_hbm.at[0], tokens_ref),
+        "w": (weights_hbm.at[0, qkv, :, head_cols], weights_ref.at[qkv, :, head_cols]),
+        "ids": (ids_hbm, ids_ref),
+        "cot": (cot_hbm.at[0], cot_ref),
+        "r": (residue_hbm.at[0, 3, head], residue_ref.at[3, head]),
+        "w+": (weights_hbm.at[0, qkv, :, rest_cols], weights_ref.at[qkv, :, rest_cols]),
+        "r+": (residue_hbm.at[0, 3, rest], residue_ref.at[3, rest]),
+        "w3": (weights_hbm.at[0, 3], weights_ref.at[3]),
+        "r2": (residue_hbm.at[0, 2], residue_ref.at[2]),
+        "r01": (residue_hbm.at[0, pair], residue_ref.at[pair]),
+    }
+    loads = {}
+    for n, (name, move) in enumerate(moves.items()):
+        loads[name] = pltpu.make_async_copy(*move, load_sems.at[n])
         loads[name].start()
 
-    def track_copy(c):
+    barrier = pltpu.get_barrier_semaphore()
+    for other in [target, source] + partners:
+        pl.semaphore_signal(barrier, inc=1, device_id=(other,), device_id_type=MESH)
+
+    def track_copy(n, c, size=1):
+        at = pl.ds(c, size)
         return pltpu.make_async_remote_copy(
-            tracked.at[c], tracked_in.at[c], track_send.at[c], track_recv.at[c], (target,), MESH
+            tracked.at[at],
+            tracked_in.at[at],
+            track_send.at[n],
+            track_recv.at[c // per_matrix],
+            (target,),
+            MESH,
         )
 
-    def sent_copy(c):
+    def slot(c):
+        return 0 if mutual or c < per_matrix else 1 + c % per_matrix
+
+    def sent_sem(m, c):
+        first = order.index(m)
+        return first if first < matrices - 1 else c - first * (per_matrix - 1)
+
+    def sent_copy(m, c):
         return pltpu.make_async_remote_copy(
-            sent.at[c], sent_in.at[c], sent_send.at[c], sent_recv.at[c], (target,), MESH
+            sent.at[c], sent_in.at[c], sent_send.at[0], sent_recv.at[sent_sem(m, c)], (target,), MESH
         )
 
     def weights_copy(m, part, c):
         return pltpu.make_async_remote_copy(
             weights_hbm.at[0, m, part],
             sent_in.at[c],
-            sent_send.at[c],
-            sent_recv.at[c],
+            sent_send.at[0],
+            sent_recv.at[sent_sem(m, c)],
             (target,),
             MESH,
         )
+
+    def sent_span(c, size, sem):
+        at = pl.ds(c, size)
+        return pltpu.make_async_remote_copy(
+            sent.at[at], sent_in.at[at], sent_send.at[0], sent_recv.at[sem], (target,), MESH
+        )
+
+    def await_tracked(m):
+        track_copy(0, order.index(m) * per_matrix, per_matrix).wait_recv()
+
+    def await_sent(m):
+        first = order.index(m)
+        if first < matrices - 1:
+            sent_span(first * per_matrix, per_matrix, first).wait_recv()
+
+    def await_last(m, c):
+        if order.index(m) == matrices - 1:
+            sent_span(c, 1, sent_sem(m, c)).wait_recv()
 
     def each_block(which, body):
         for m in which:
@@ -159,8 +195,10 @@
         grad = dot(left_ref[m // 3, part], right) * proj_scale
         gradient[c] = grad
         tracked[c] = (residue_ref[m, part].astype(f32) + grad).astype(bf16)
-        if mutual or m in order[:2]:
-            track_copy(c).start()
+        if mutual or m == order[0]:
+            track_copy(0, c).start()
+        elif m == order[1]:
+            track_copy(1 + c - per_matrix, c).start()
         squares[...] += jnp.sum((grad * grad).reshape(-1, 8, width), 0)
 
     loads["ids"].wait()
@@ -173,8 +211,7 @@
     for j in range(pairs):
         cols = slice(j * LANES, (j + 1) * LANES)
         if j < 2:
-            for m in range(3):
-                loads["w+" if j else "w", m].wait()
+            loads["w+" if j else "w"].wait()
         queries, keys, vals = [
             (dot(normed, weights_ref[m, :, cols]) * proj_scale).astype(bf16) for m in range(3)
         ]
@@ -192,10 +229,10 @@
         if j == 0 and not mutual:
             pl.semaphore_wait(barrier, 2 + steps)
         if j < 2:
-            loads["r+" if j else "r", 3].wait()
+            loads["r+" if j else "r"].wait()
         track(3, pl.ds(j * LANES, LANES), order.index(3) * per_matrix + j)
 
-    loads["w", 3].wait()
+    loads["w3"].wait()
     context_grad = (dot(cot, weights_ref[3], 1, 1) * proj_scale).astype(bf16)
     weighted = [unit_rows[i * seq : (i + 1) * seq] * counts[i] for i in range(pool)]
     left_ref[0] = jnp.concatenate(weighted, 0).T.astype(bf16)
@@ -205,7 +242,7 @@
     grads2 = [spread(context_grad[at]) for at in spots]
     for n, at in enumerate(spots):
         right_ref[2, at[0], at[1]] = dot(half[n], grads2[n], 0, 0).astype(bf16)
-    loads["r", 2].wait()
+    loads["r2"].wait()
     each_block([2], track)
     probs_grad = [dot(g, v, 1, 1) for g, v in zip(grads2, vals1)]
     score_grad = []
@@ -215,13 +252,12 @@
     for n, at in enumerate(spots):
         right_ref[0, at[0], at[1]] = gather(dot(score_grad[n], keys1[n])).astype(bf16)
         right_ref[1, at[0], at[1]] = dot(score_grad[n], queries2[n], 0, 0).astype(bf16)
-    for m in order[2:]:
-        loads["r", m].wait()
+    loads["r01"].wait()
     each_block(order[2:], track)
 
     def sum_copy(k):
         return pltpu.make_async_remote_copy(
-            totals.at[k], totals_in.at[k], sum_send.at[k], sum_recv.at[k], (partners[k],), MESH
+            totals.at[k], totals_in.at[k], sum_send.at[0], sum_recv.at[k], (partners[k],), MESH
         )
 
     def sum_finish(k):
@@ -236,30 +272,29 @@
         rms_ref[0] = jnp.sqrt(totals[steps] / entries)
 
     def mix(m, part, c):
-        track_copy(c).wait_recv()
         tracker = 0.5 * (tracked[c].astype(f32) + tracked_in[c].astype(f32))
         own = weights_ref[m, part].astype(f32)
         new_residue_ref[0, m, part] = (tracker - gradient[c]).astype(bf16)
         base = 0.5 * own - 0.5 * step_rate * tracker
         if mutual:
-            weights_copy(m, part, c).wait_recv()
+            await_last(m, c)
             peer_sent = (sent_in[c].astype(f32) - step_rate * tracker).astype(bf16)
             new_weights_ref[0, m, part] = (base + 0.5 * peer_sent.astype(f32)).astype(bf16)
         else:
             sent[c] = (own - step_rate * tracker).astype(bf16)
-            sent_copy(c).start()
+            sent_copy(m, c).start()
             gradient[c] = base
 
+    def mix_all(which):
+        for m in which:
+            await_tracked(m)
+            if mutual:
+                await_sent(m)
+            each_block([m], mix)
+
     def finish(m, part, c):
-        sent_copy(c).wait_recv()
+        await_last(m, c)
         new_weights_ref[0, m, part] = (gradient[c] + 0.5 * sent_in[c].astype(f32)).astype(bf16)
-
-    def drain(m, part, c):
-        track_copy(c).wait_send()
-        weights_copy(m, part, c).wait_send()
-
-    def drain_sent(m, part, c):
-        sent_copy(c).wait_send()
 
     if mutual:
         for k in range(steps - 2):
@@ -268,39 +303,43 @@
         for n, k in enumerate([steps - 2, steps - 1]):
             sum_copy(k).start()
             each_block([order[2 + n]], send_weights)
-            each_block([order[n]], mix)
+            mix_all([order[n]])
             sum_finish(k)
         set_rms()
-        each_block(order[2:], mix)
-        each_block(order, drain)
+        mix_all(order[2:])
+        track_copy(0, 0, chunks).wait_send()
     else:
-        chunks = matrices * per_matrix
         held = 2 * per_matrix
-        lag = min(3, held)
         starts = [held + k * (chunks - held) // steps for k in range(steps)]
+        gone = per_matrix
         for c in range(held, chunks):
-            track_copy(c - lag).wait_send()
+            while gone <= c - LAG:
+                track_copy(slot(gone), gone).wait_send()
+                gone += 1
             for k in range(steps):
                 if starts[k] == c:
                     if k:
                         sum_finish(k - 1)
                     sum_copy(k).start()
-            track_copy(c).start()
+            track_copy(slot(c), c).start()
         sum_finish(steps - 1)
         set_rms()
-        each_block(order, mix)
-        each_block(order, finish)
-        for c in range(chunks):
-            if c < held - lag or c >= chunks - lag:
-                track_copy(c).wait_send()
-        each_block(order, drain_sent)
+        mix_all(order)
+        for m in order:
+            await_sent(m)
+            each_block([m], finish)
+        track_copy(0, 0, per_matrix).wait_send()
+        for c in range(gone, chunks):
+            track_copy(slot(c), c).wait_send()
+    sent_span(0, chunks, 0).wait_send()
 
 
 def one_round(nodes, level, sample_ids, token_pool, cotangent_pool, weights, residue):
     pool, seq, width = token_pool.shape[1:]
     matrices = weights.shape[1]
     rows = pool * seq
-    chunks = matrices * (width // CHUNK_ROWS)
+    per_matrix = width // CHUNK_ROWS
+    chunks = matrices * per_matrix
     steps = nodes.bit_length() - 1
     chunked = (chunks, CHUNK_ROWS, width)
     dma = pltpu.SemaphoreType.DMA
@@ -330,12 +369,12 @@
             pltpu.VMEM((8, width), f32),
             pltpu.VMEM((steps + 1, 8, LANES), f32),
             pltpu.VMEM((steps, 8, LANES), f32),
-            dma((7 + 2 * matrices,)),
-            dma((chunks,)),
-            dma((chunks,)),
-            dma((chunks,)),
-            dma((chunks,)),
-            dma((steps,)),
+            dma((10,)),
+            dma((1 + per_matrix,)),
+            dma((matrices,)),
+            dma((1,)),
+            dma((matrices - 1 + per_matrix,)),
+            dma((1,)),
             dma((steps,)),
         ],
         compiler_params=pltpu.CompilerParams(

time: 104 us -> 104 us (level)
  no operation moved by 1% of the time
where the time goes in v2:
time: 104 us
  Pallas kernels  102 us (98%)
  between operations  1.48 us (1%)
    pallas_call x1, Pallas kernels, one_round(): pl.pallas_call(partial(round_kernel, nodes, 2 ** level), out_shape=(jax.S...  100 us
    pallas_call x1, Pallas kernels, write_out(): pl.pallas_call(write_kernel, out_shape=(shape, shape, jax.ShapeDtypeStruc...  2.09 us

profile of v2, /device:TPU:0, one launch (start us, length us, event | category | flops | bytes accessed | tf_op | source)
XLA Modules:
  0.0 104.2 jit_solution(14961479881782009033)
XLA Ops:
  1.3 100.7 %conditional.1 = (bf16[1,4,512,512]{3,2,1,0:T(8,128)(2,1)S(1)}, bf16[1,4,512,512]{3,2,1,0:T(8,128)(2,1)S(1)}, f32[8,128]{1,0:T(8,128)S(1)}) conditional(s32[]{:T(128)} %clamp.3, (s32[1,8]{1,0:T(1,128)}, bf16[1,4,64,512]{3,2,1,0:T(8,128)(2,1)}, bf16[1,4,64,512]{3,2,1,0:T(8,128)(2,1)}, ...), branch_computations={%region_0.1_spmd, %region_1.2_spmd, %region_2.3_spmd, %region_3.4_... | conditional | bytes 24 | solution.py:417
  1.3 100.4 %branch_1_fun.1 = (bf16[1,4,512,512]{3,2,1,0:T(8,128)(2,1)S(1)}, bf16[1,4,512,512]{3,2,1,0:T(8,128)(2,1)S(1)}, f32[1,8,128]{2,1,0:T(8,128)S(1)}) custom-call(s32[1,8]{1,0:T(1,128)} %get-tuple-element.58.ids_hbm, bf16[1,4,64,512]{3,2,1,0:T(8,128)(2,1)} %get-tuple-element.59.tokens_hbm, bf16[1,4,64,512]{3,2,1,0:T(8,128)(2,1)} %get-tuple-element.60.cot_hbm, ...), custom_call_target="tpu_custom_call" | custom-call | tf_op jit(solution)/shard_map/cond/branch_1_fun/pallas_call | solution.py:346
  102.0 2.1 %shard_map.85 = (bf16[1,4,512,512]{3,2,1,0:T(8,128)(2,1)}, bf16[1,4,512,512]{3,2,1,0:T(8,128)(2,1)}, f32[1]{0:T(128)}) custom-call(bf16[1,4,512,512]{3,2,1,0:T(8,128)(2,1)S(1)} %get-tuple-element.99.weights_ref, bf16[1,4,512,512]{3,2,1,0:T(8,128)(2,1)S(1)} %get-tuple-element.100.residue_ref, f32[8,128]{1,0:T(8,128)S(1)} %get-tuple-element.101.rms_ref), custom_call_target="tpu_custom_call" | custom-call | tf_op jit(solution)/shard_map/pallas_call | solution.py:404

commit v3 on v2

--- a/solution.py
+++ b/solution.py
@@ -311,17 +311,30 @@
     else:
         held = 2 * per_matrix
         starts = [held + k * (chunks - held) // steps for k in range(steps)]
-        gone = per_matrix
-        for c in range(held, chunks):
-            while gone <= c - LAG:
-                track_copy(slot(gone), gone).wait_send()
-                gone += 1
-            for k in range(steps):
-                if starts[k] == c:
-                    if k:
-                        sum_finish(k - 1)
-                    sum_copy(k).start()
-            track_copy(slot(c), c).start()
+
+        def hand_out(lag):
+            gone = per_matrix
+            for c in range(held, chunks):
+                while gone <= c - (lag if c >= chunks - per_matrix else LAG):
+                    track_copy(slot(gone), gone).wait_send()
+                    gone += 1
+                for k in range(steps):
+                    if starts[k] == c:
+                        if k:
+                            sum_finish(k - 1)
+                        sum_copy(k).start()
+                track_copy(slot(c), c).start()
+        if offset == 1:
+            hand_out(LAG)
+        else:
+            @pl.when(me % 2 == 0)
+            def _():
+                hand_out(LAG)
+
+            @pl.when(me % 2 == 1)
+            def _():
+                hand_out(1)
+
         sum_finish(steps - 1)
         set_rms()
         mix_all(order)
@@ -329,8 +342,16 @@
             await_sent(m)
             each_block([m], finish)
         track_copy(0, 0, per_matrix).wait_send()
-        for c in range(gone, chunks):
-            track_copy(slot(c), c).wait_send()
+
+        def await_gone(lag):
+            for c in range(chunks - lag, chunks):
+                track_copy(slot(c), c).wait_send()
+
+        if offset == 1:
+            await_gone(LAG)
+        else:
+            pl.when(me % 2 == 0)(lambda: await_gone(LAG))
+            pl.when(me % 2 == 1)(lambda: await_gone(1))
     sent_span(0, chunks, 0).wait_send()
 
 

time: 104 us -> 103 us (level)
  Pallas kernels: 102 us -> 100 us
    pallas_call x1, Pallas kernels: 100 us -> 98.3 us  [one_round(): pl.pallas_call(partial(round_kernel, nodes, 2 ** level), out_shape=(jax.S...]
where the time goes in v3:
time: 103 us
  Pallas kernels  100 us (97%)
  between operations  1.48 us (1%)
    pallas_call x1, Pallas kernels, one_round(): pl.pallas_call(partial(round_kernel, nodes, 2 ** level), out_shape=(jax.S...  98.3 us
    pallas_call x1, Pallas kernels, write_out(): pl.pallas_call(write_kernel, out_shape=(shape, shape, jax.ShapeDtypeStruc...  2.09 us

profile of v3, /device:TPU:0, one launch (start us, length us, event | category | flops | bytes accessed | tf_op | source)
XLA Modules:
  0.0 102.6 jit_solution(9128979871278965236)
XLA Ops:
  1.3 99.0 %conditional.1 = (bf16[1,4,512,512]{3,2,1,0:T(8,128)(2,1)S(1)}, bf16[1,4,512,512]{3,2,1,0:T(8,128)(2,1)S(1)}, f32[8,128]{1,0:T(8,128)S(1)}) conditional(s32[]{:T(128)} %clamp.3, (s32[1,8]{1,0:T(1,128)}, bf16[1,4,64,512]{3,2,1,0:T(8,128)(2,1)}, bf16[1,4,64,512]{3,2,1,0:T(8,128)(2,1)}, ...), branch_computations={%region_0.1_spmd, %region_1.2_spmd, %region_2.3_spmd, %region_3.4_... | conditional | bytes 24 | solution.py:438
  1.5 98.3 %branch_2_fun.1 = (bf16[1,4,512,512]{3,2,1,0:T(8,128)(2,1)S(1)}, bf16[1,4,512,512]{3,2,1,0:T(8,128)(2,1)S(1)}, f32[1,8,128]{2,1,0:T(8,128)S(1)}) custom-call(s32[1,8]{1,0:T(1,128)} %get-tuple-element.66.ids_hbm, bf16[1,4,64,512]{3,2,1,0:T(8,128)(2,1)} %get-tuple-element.67.tokens_hbm, bf16[1,4,64,512]{3,2,1,0:T(8,128)(2,1)} %get-tuple-element.68.cot_hbm, ...), custom_call_target="tpu_custom_call" | custom-call | tf_op jit(solution)/shard_map/cond/branch_2_fun/pallas_call | solution.py:367
  100.3 2.1 %shard_map.85 = (bf16[1,4,512,512]{3,2,1,0:T(8,128)(2,1)}, bf16[1,4,512,512]{3,2,1,0:T(8,128)(2,1)}, f32[1]{0:T(128)}) custom-call(bf16[1,4,512,512]{3,2,1,0:T(8,128)(2,1)S(1)} %get-tuple-element.99.weights_ref, bf16[1,4,512,512]{3,2,1,0:T(8,128)(2,1)S(1)} %get-tuple-element.100.residue_ref, f32[8,128]{1,0:T(8,128)S(1)} %get-tuple-element.101.rms_ref), custom_call_target="tpu_custom_call" | custom-call | tf_op jit(solution)/shard_map/pallas_call | solution.py:425

commit v4 on v2

--- a/solution.py
+++ b/solution.py
@@ -80,7 +80,8 @@
     chunks = matrices * per_matrix
     proj_scale = width**-0.5
     head_scale = HEAD_DIM**-0.5
-    order = [3, 2, 0, 1]
+    last = matrices - 1
+    tail = last * per_matrix
 
     head, rest = pl.ds(0, CHUNK_ROWS), pl.ds(CHUNK_ROWS, width - CHUNK_ROWS)
     head_cols, rest_cols = pl.ds(0, LANES), pl.ds(LANES, width - LANES)
@@ -118,58 +119,44 @@
         )
 
     def slot(c):
-        return 0 if mutual or c < per_matrix else 1 + c % per_matrix
-
-    def sent_sem(m, c):
-        first = order.index(m)
-        return first if first < matrices - 1 else c - first * (per_matrix - 1)
-
-    def sent_copy(m, c):
+        return 0 if mutual else 1 + c % per_matrix
+
+    def sent_sem(c):
+        return c // per_matrix + (c % per_matrix) * (c // tail)
+
+    def sent_copy(c, size=1):
+        at = pl.ds(c, size)
         return pltpu.make_async_remote_copy(
-            sent.at[c], sent_in.at[c], sent_send.at[0], sent_recv.at[sent_sem(m, c)], (target,), MESH
+            sent.at[at], sent_in.at[at], sent_send.at[0], sent_recv.at[sent_sem(c)], (target,), MESH
         )
 
-    def weights_copy(m, part, c):
-        return pltpu.make_async_remote_copy(
+    def send_weights(m, part, c):
+        pltpu.make_async_remote_copy(
             weights_hbm.at[0, m, part],
             sent_in.at[c],
             sent_send.at[0],
-            sent_recv.at[sent_sem(m, c)],
+            sent_recv.at[sent_sem(c)],
             (target,),
             MESH,
-        )
-
-    def sent_span(c, size, sem):
-        at = pl.ds(c, size)
-        return pltpu.make_async_remote_copy(
-            sent.at[at], sent_in.at[at], sent_send.at[0], sent_recv.at[sem], (target,), MESH
-        )
-
-    def await_tracked(m):
-        track_copy(0, order.index(m) * per_matrix, per_matrix).wait_recv()
-
-    def await_sent(m):
-        first = order.index(m)
-        if first < matrices - 1:
-            sent_span(first * per_matrix, per_matrix, first).wait_recv()
-
-    def await_last(m, c):
-        if order.index(m) == matrices - 1:
-            sent_span(c, 1, sent_sem(m, c)).wait_recv()
-
-    def each_block(which, body):
-        for m in which:
-
-            @pl.loop(0, per_matrix)
-            def _(r):
-                body(m, pl.ds(r * CHUNK_ROWS, CHUNK_ROWS), order.index(m) * per_matrix + r)
-
-    def send_weights(m, part, c):
-        weights_copy(m, part, c).start()
+        ).start()
+
+    def await_sent(c):
+        @pl.when(c >= tail)
+        def _():
+            sent_copy(c).wait_recv()
+
+        @pl.when((c < tail) & (c % per_matrix == 0))
+        def _():
+            sent_copy(c, per_matrix).wait_recv()
+
+    def each_block(first, end, body):
+        @pl.loop(first * per_matrix, end * per_matrix)
+        def _(c):
+            body(last - c // per_matrix, pl.ds((c % per_matrix) * CHUNK_ROWS, CHUNK_ROWS), c)
 
     if mutual:
         pl.semaphore_wait(barrier, 2 + steps)
-        each_block(order[:2], send_weights)
+        each_block(0, 2, send_weights)
 
     loads["tokens"].wait()
     values = tokens_ref[...].reshape(rows, width).astype(f32)
@@ -190,16 +177,20 @@
     def gather(block):
         return jnp.where(first, block[:seq], block[seq:])
 
-    def track(m, part, c):
-        right = right_ref[m] if m < 3 else cot
-        grad = dot(left_ref[m // 3, part], right) * proj_scale
+    def track(left, right, m, part, c):
+        grad = dot(left, right) * proj_scale
         gradient[c] = grad
         tracked[c] = (residue_ref[m, part].astype(f32) + grad).astype(bf16)
-        if mutual or m == order[0]:
-            track_copy(0, c).start()
-        elif m == order[1]:
-            track_copy(1 + c - per_matrix, c).start()
         squares[...] += jnp.sum((grad * grad).reshape(-1, 8, width), 0)
+
+    def track_value(m, part, c):
+        track(left_ref[0, part], right_ref[2], m, part, c)
+        track_copy(slot(c), c).start()
+
+    def track_rest(m, part, c):
+        track(left_ref[0, part], right_ref[m], m, part, c)
+        if mutual:
+            track_copy(slot(c), c).start()
 
     loads["ids"].wait()
     ids = ids_ref[...]
@@ -212,6 +203,7 @@
         cols = slice(j * LANES, (j + 1) * LANES)
         if j < 2:
             loads["w+" if j else "w"].wait()
+            loads["r+" if j else "r"].wait()
         queries, keys, vals = [
             (dot(normed, weights_ref[m, :, cols]) * proj_scale).astype(bf16) for m in range(3)
         ]
@@ -225,12 +217,12 @@
             probs[u] = e / jnp.sum(e, -1, keepdims=True)
             half[u] = probs[u].astype(bf16)
         context = [gather(dot(half[u], vals1[u])) * counts[u[0]] for u in here]
-        left_ref[1, cols] = jnp.concatenate(context, 0).T.astype(bf16)
+        left_ref[1, cols] = jnp.concatenate(context, 0).astype(bf16).T
         if j == 0 and not mutual:
             pl.semaphore_wait(barrier, 2 + steps)
-        if j < 2:
-            loads["r+" if j else "r"].wait()
-        track(3, pl.ds(j * LANES, LANES), order.index(3) * per_matrix + j)
+        part = pl.ds(j * LANES, LANES)
+        track(left_ref[1, part], cot, last, part, j)
+        track_copy(0, j).start()
 
     loads["w3"].wait()
     context_grad = (dot(cot, weights_ref[3], 1, 1) * proj_scale).astype(bf16)
@@ -243,7 +235,7 @@
     for n, at in enumerate(spots):
         right_ref[2, at[0], at[1]] = dot(half[n], grads2[n], 0, 0).astype(bf16)
     loads["r2"].wait()
-    each_block([2], track)
+    each_block(1, 2, track_value)
     probs_grad = [dot(g, v, 1, 1) for g, v in zip(grads2, vals1)]
     score_grad = []
     for p, g in zip(probs, probs_grad):
@@ -253,7 +245,7 @@
         right_ref[0, at[0], at[1]] = gather(dot(score_grad[n], keys1[n])).astype(bf16)
         right_ref[1, at[0], at[1]] = dot(score_grad[n], queries2[n], 0, 0).astype(bf16)
     loads["r01"].wait()
-    each_block(order[2:], track)
+    each_block(2, matrices, track_rest)
 
     def sum_copy(k):
         return pltpu.make_async_remote_copy(
@@ -272,29 +264,29 @@
         rms_ref[0] = jnp.sqrt(totals[steps] / entries)
 
     def mix(m, part, c):
+        @pl.when(c % per_matrix == 0)
+        def _():
+            track_copy(0, c, per_matrix).wait_recv()
+
         tracker = 0.5 * (tracked[c].astype(f32) + tracked_in[c].astype(f32))
         own = weights_ref[m, part].astype(f32)
         new_residue_ref[0, m, part] = (tracker - gradient[c]).astype(bf16)
         base = 0.5 * own - 0.5 * step_rate * tracker
         if mutual:
-            await_last(m, c)
+            await_sent(c)
             peer_sent = (sent_in[c].astype(f32) - step_rate * tracker).astype(bf16)
             new_weights_ref[0, m, part] = (base + 0.5 * peer_sent.astype(f32)).astype(bf16)
         else:
             sent[c] = (own - step_rate * tracker).astype(bf16)
-            sent_copy(m, c).start()
+            sent_copy(c).start()
             gradient[c] = base
 
-    def mix_all(which):
-        for m in which:
-            await_tracked(m)
-            if mutual:
-                await_sent(m)
-            each_block([m], mix)
-
     def finish(m, part, c):
-        await_last(m, c)
+        await_sent(c)
         new_weights_ref[0, m, part] = (gradient[c] + 0.5 * sent_in[c].astype(f32)).astype(bf16)
+
+    def await_gone(c):
+        track_copy(slot(c), c).wait_send()
 
     if mutual:
         for k in range(steps - 2):
@@ -302,20 +294,28 @@
             sum_finish(k)
         for n, k in enumerate([steps - 2, steps - 1]):
             sum_copy(k).start()
-            each_block([order[2 + n]], send_weights)
-            mix_all([order[n]])
+            each_block(2 + n, 3 + n, send_weights)
+            each_block(n, n + 1, mix)
             sum_finish(k)
         set_rms()
-        mix_all(order[2:])
+        each_block(2, matrices, mix)
         track_copy(0, 0, chunks).wait_send()
     else:
+        second = 0 if offset == 1 else me % 2
+        ahead = second * (LAG - 1)
         held = 2 * per_matrix
         starts = [held + k * (chunks - held) // steps for k in range(steps)]
-        gone = per_matrix
+        for gone in range(per_matrix, held - LAG):
+            await_gone(gone)
         for c in range(held, chunks):
-            while gone <= c - LAG:
-                track_copy(slot(gone), gone).wait_send()
-                gone += 1
+            await_gone(c - LAG if c <= tail else c - LAG + ahead)
+            if c == tail:
+
+                @pl.when(second == 1)
+                def _():
+                    for gone in range(c - LAG + 1, c):
+                        await_gone(gone)
+
             for k in range(steps):
                 if starts[k] == c:
                     if k:
@@ -324,14 +324,17 @@
             track_copy(slot(c), c).start()
         sum_finish(steps - 1)
         set_rms()
-        mix_all(order)
-        for m in order:
-            await_sent(m)
-            each_block([m], finish)
+        each_block(0, matrices, mix)
+        each_block(0, matrices, finish)
         track_copy(0, 0, per_matrix).wait_send()
-        for c in range(gone, chunks):
-            track_copy(slot(c), c).wait_send()
-    sent_span(0, chunks, 0).wait_send()
+
+        @pl.when(second == 0)
+        def _():
+            for gone in range(chunks - LAG, chunks - 1):
+                await_gone(gone)
+
+        await_gone(chunks - 1)
+    sent_copy(0, chunks).wait_send()
 
 
 def one_round(nodes, level, sample_ids, token_pool, cotangent_pool, weights, residue):

time: 104 us -> 102 us (0.981)
  Pallas kernels: 102 us -> 99.4 us
    pallas_call x1, Pallas kernels: 100 us -> 97.4 us  [one_round(): pl.pallas_call(partial(round_kernel, nodes, 2 ** level), out_shape=(jax.S...]
where the time goes in v4:
time: 102 us; the launch traced here: 101 us
  Pallas kernels  99.4 us (97%)
  between operations  1.48 us (1%)
    pallas_call x1, Pallas kernels, one_round(): pl.pallas_call(partial(round_kernel, nodes, 2 ** level), out_shape=(jax.S...  97.4 us
    pallas_call x1, Pallas kernels, write_out(): pl.pallas_call(write_kernel, out_shape=(shape, shape, jax.ShapeDtypeStruc...  2.09 us

profile of v4, /device:TPU:0, one launch (start us, length us, event | category | flops | bytes accessed | tf_op | source)
XLA Modules:
  0.0 101.4 jit_solution(4150829383629260303)
XLA Ops:
  1.3 97.8 %conditional.1 = (bf16[1,4,512,512]{3,2,1,0:T(8,128)(2,1)S(1)}, bf16[1,4,512,512]{3,2,1,0:T(8,128)(2,1)S(1)}, f32[8,128]{1,0:T(8,128)S(1)}) conditional(s32[]{:T(128)} %clamp.3, (s32[1,8]{1,0:T(1,128)}, bf16[1,4,64,512]{3,2,1,0:T(8,128)(2,1)}, bf16[1,4,64,512]{3,2,1,0:T(8,128)(2,1)}, ...), branch_computations={%region_0.1_spmd, %region_1.2_spmd, %region_2.3_spmd, %region_3.4_... | conditional | bytes 24 | solution.py:420
  1.5 97.4 %branch_3_fun.1 = (bf16[1,4,512,512]{3,2,1,0:T(8,128)(2,1)S(1)}, bf16[1,4,512,512]{3,2,1,0:T(8,128)(2,1)S(1)}, f32[1,8,128]{2,1,0:T(8,128)S(1)}) custom-call(s32[1,8]{1,0:T(1,128)} %get-tuple-element.74.ids_hbm, bf16[1,4,64,512]{3,2,1,0:T(8,128)(2,1)} %get-tuple-element.75.tokens_hbm, bf16[1,4,64,512]{3,2,1,0:T(8,128)(2,1)} %get-tuple-element.76.cot_hbm, ...), custom_call_target="tpu_custom_call" | custom-call | tf_op jit(solution)/shard_map/cond/branch_3_fun/pallas_call | solution.py:349
  99.1 2.1 %shard_map.85 = (bf16[1,4,512,512]{3,2,1,0:T(8,128)(2,1)}, bf16[1,4,512,512]{3,2,1,0:T(8,128)(2,1)}, f32[1]{0:T(128)}) custom-call(bf16[1,4,512,512]{3,2,1,0:T(8,128)(2,1)S(1)} %get-tuple-element.99.weights_ref, bf16[1,4,512,512]{3,2,1,0:T(8,128)(2,1)S(1)} %get-tuple-element.100.residue_ref, f32[8,128]{1,0:T(8,128)S(1)} %get-tuple-element.101.rms_ref), custom_call_target="tpu_custom_call" | custom-call | tf_op jit(solution)/shard_map/pallas_call | solution.py:407
